TPU v7x, 32 devices: a whole 2x2x4 slice. The times are simulated.
32 devices in a mesh: data: 2 (over x), pp: 4 (over z), ep: 4 (over y, core).
Axes of the slice: x: 2, y: 2, z: 4, core: 2. Of those that a mesh axis runs over, the one named last changes fastest.
Arguments:
- O: bfloat16 [8, 6, 64, 96, 1792], P(('data', 'pp'), None, 'ep'), parts along dimension 0
- idx: int32 [8, 6, 4, 128, 8], P(('data', 'pp'), None, 'ep'), parts along dimension 0
- slot: int32 [8, 6, 4, 128, 8], P(('data', 'pp'), None, 'ep'), parts along dimension 0
- g: float32 [8, 6, 4, 128, 8], P(('data', 'pp'), None, 'ep'), parts along dimension 0
- H: bfloat16 [8, 6, 4, 128, 1792], P(('data', 'pp'), None, 'ep'), parts along dimension 0
- w: float32 [4, 1792], P('pp')
- Wq: bfloat16 [4, 1792, 32, 128], P('pp')
- Wk: bfloat16 [4, 1792, 32, 128], P('pp')
- Wv: bfloat16 [4, 1792, 32, 128], P('pp')
- Wo: bfloat16 [4, 32, 128, 1792], P('pp')
Outputs:
- output: bfloat16 [8, 6, 4, 128, 1792], P(('data', 'pp'), None, 'ep'), parts along dimension 0
There are 2 independent parts. A program takes and returns all parts, laid end to end along the dimension named above; an argument that names none is the same for every part.
All inputs are finite; a program needn't handle non-finite values.
Results may differ from a plain program's by a relative error of at most 0.0128283.
Values are sent between devices in bfloat16 or wider.
A program may use at most 1 GiB of HBM per device.

v0:
```python
import jax
import jax.numpy as jnp
from jax import lax
from jax.experimental import pallas as pl
from jax.experimental.pallas import tpu as pltpu
from jax.sharding import PartitionSpec as P


EPS = 1e-6
F32 = jnp.float32
BF16 = jnp.bfloat16
NT = (((1,), (1,)), ((), ()))
VMEM_LIMIT = 60 * 2**20
HS = 4


def gate_terms(pos, gate, g_s, slot):
    t = pos.shape[1]
    rows = g_s.shape[2]
    col = lax.broadcasted_iota(jnp.int32, (t, rows), 1).astype(F32)
    pt = pos.T
    gt = gate.T
    acc = jnp.zeros((t, rows), F32)
    for j in range(pos.shape[0]):
        acc = jnp.where(pt[:, j:j + 1] == col, gt[:, j:j + 1], acc)
    hi = acc.astype(BF16)
    rest = acc - hi.astype(F32)
    mid = rest.astype(BF16)
    g_s[slot, 0:t] = hi
    g_s[slot, t:2 * t] = mid
    g_s[slot, 2 * t:3 * t] = (rest - mid.astype(F32)).astype(BF16)


def front_kernel(sent_ref, here_ref, o_ref, part_ref, *rest):
    n_mb = sent_ref.shape[0]
    far_refs, (near_ref, pg, rows, sums, g_s, own_sem, row_send, row_recv, pg_sem, y_sem, out_sem) = rest[:n_mb - 1], rest[n_mb - 1:]
    n_ep = o_ref.shape[2]
    d = o_ref.shape[-1]
    t = g_s.shape[1] // 3
    e = lax.axis_index('ep')
    mate = e + 1 - 2 * lax.rem(e, 2)
    across = lax.rem(e + 2, n_ep)
    mate_across = lax.rem(mate + 2, n_ep)

    barrier = pltpu.get_barrier_semaphore()
    for dev in (mate, across):
        pl.semaphore_signal(barrier, inc=1, device_id={'ep': dev}, device_id_type=pl.DeviceIdType.MESH)
    pl.semaphore_wait(barrier, 2)

    gates = pltpu.make_async_remote_copy(sent_ref, pg.at[pl.ds(0, n_mb)], pg_sem.at[0], pg_sem.at[1],
                                         device_id={'ep': across}, device_id_type=pl.DeviceIdType.MESH)
    gates.start()
    own, got = [], []
    for i in range(2 * n_mb):
        m = i % n_mb
        mine, theirs = (across, mate_across) if i < n_mb else (e, mate)
        got.append(pltpu.make_async_remote_copy(o_ref.at[m, :, theirs], rows.at[i, 1], row_send.at[i], row_recv.at[i],
                                                device_id={'ep': mate}, device_id_type=pl.DeviceIdType.MESH))
        own.append(pltpu.make_async_copy(o_ref.at[m, :, mine], rows.at[i, 0], own_sem.at[i]))
        got[i].start()
        own[i].start()
    pg[n_mb:] = here_ref[...]
    gates.wait()

    def wait_rows(i):
        pltpu.make_async_copy(o_ref.at[0, :, 0], rows.at[i, 0], own_sem.at[i]).wait()
        pltpu.make_async_remote_copy(o_ref.at[0, :, 0], rows.at[i, 1], row_send.at[i], row_recv.at[i],
                                     device_id={'ep': mate}, device_id_type=pl.DeviceIdType.MESH).wait()

    def gates_of(i):
        gate_terms(pg[i, :8], pg[i, 8:], g_s, lax.rem(i, 2))

    def one(i, _):
        wait_rows(i)
        slot = lax.rem(i, 2)
        gates_of(lax.rem(i + 1, 2 * n_mb))
        for n in range(d // 256):
            c = slice(n * 256, (n + 1) * 256)
            r = jnp.dot(g_s[slot], rows[i, :, :, :, c].reshape(g_s.shape[2], 256), preferred_element_type=F32)
            sums[i, :, c] = (r[2 * t:] + r[t:2 * t]) + r[:t]
        return 0

    gates_of(0)
    one(0, 0)
    first = pltpu.make_async_remote_copy(sums.at[0], part_ref, y_sem.at[0], y_sem.at[1],
                                         device_id={'ep': across}, device_id_type=pl.DeviceIdType.MESH)
    first.start()
    lax.fori_loop(1, n_mb, one, 0)
    outs = [pltpu.make_async_copy(sums.at[m], far_refs[m - 1], out_sem.at[m]) for m in range(1, n_mb)]
    for c in outs:
        c.start()
    lax.fori_loop(n_mb, 2 * n_mb, one, 0)
    near = pltpu.make_async_copy(sums.at[pl.ds(n_mb, n_mb)], near_ref, out_sem.at[0])
    near.start()
    for c in outs + [near]:
        c.wait()
    first.wait()


def front(sent, here, o5):
    mb, ne, _, cg, d = o5.shape
    t = sent.shape[2]
    one = jax.ShapeDtypeStruct((t, d), F32)
    any_ = pl.BlockSpec(memory_space=pl.ANY)
    vm = pl.BlockSpec(memory_space=pltpu.VMEM)
    dma = pltpu.SemaphoreType.DMA
    return pl.pallas_call(
        front_kernel, name="front",
        in_specs=[vm, vm, any_], out_specs=[any_] * (mb + 1),
        out_shape=[one] * mb + [jax.ShapeDtypeStruct((mb, t, d), F32)],
        scratch_shapes=[pltpu.VMEM((2 * mb,) + sent.shape[1:], F32), pltpu.VMEM((2 * mb, 2, ne, cg, d), BF16),
                        pltpu.VMEM((2 * mb, t, d), F32), pltpu.VMEM((2, 3 * t, 2 * ne * cg), BF16),
                        dma((2 * mb,)), dma((2 * mb,)), dma((2 * mb,)), dma((2,)), dma((2,)), dma((mb,))],
        cost_estimate=pl.CostEstimate(flops=2 * 3 * t * 2 * ne * cg * d * 2 * mb, bytes_accessed=0, transcendentals=0),
        compiler_params=pltpu.CompilerParams(vmem_limit_bytes=VMEM_LIMIT, collective_id=0, has_side_effects=True))(sent, here, o5)


def attn(q, k, v, nb, keep):
    hs = q.shape[1] // 128
    f = 128
    blk = [(h, b) for h in range(hs) for b in range(nb)]

    def cut(t, h, b):
        return t[b * 128:(b + 1) * 128, h * f:(h + 1) * f]

    s = [lax.dot_general(cut(q, h, b), cut(k, h, b), NT, preferred_element_type=F32) for h, b in blk]
    s = [jnp.where(keep, x * (f ** -0.5), -1e30) for x in s]
    m = [jnp.max(x, axis=-1, keepdims=True) for x in s]
    p = [jnp.exp(x - y) for x, y in zip(s, m)]
    d = [jnp.sum(x, axis=-1, keepdims=True) for x in p]
    p = [x * (1.0 / y) for x, y in zip(p, d)]
    o = [jnp.dot(x, cut(v, h, b).astype(F32), preferred_element_type=F32).astype(BF16) for x, (h, b) in zip(p, blk)]
    return jnp.concatenate([jnp.concatenate(o[h * nb:(h + 1) * nb], axis=0) for h in range(hs)], axis=1)


def turn_kernel(c_ref, q_ref, k_ref, v_ref, o_ref, qt_ref, kt_ref, vt_ref, ot_ref, sem):
    step = pl.program_id(0)
    hc = ot_ref.shape[0]
    kb = q_ref.shape[0]
    copy = pltpu.make_async_copy(o_ref.at[pl.ds(c_ref[0] * hc, hc)], ot_ref, sem)

    @pl.when(step == 0)
    def _():
        copy.start()

    rows = pl.ds(pl.multiple_of(step * kb, kb), kb)
    for i, o in ((q_ref, qt_ref), (k_ref, kt_ref), (v_ref, vt_ref)):
        o[:, rows, :] = jnp.swapaxes(i[...], 0, 1)

    @pl.when(step == pl.num_programs(0) - 1)
    def _():
        copy.wait()


def turn(core, wq, wk, wv, wo):
    d, nh, f = wq.shape
    hc, kb = nh // 2, 128
    vm = pl.BlockSpec(memory_space=pltpu.VMEM)
    return pl.pallas_call(
        turn_kernel, name="turn",
        grid_spec=pltpu.PrefetchScalarGridSpec(
            num_scalar_prefetch=1, grid=(d // kb,),
            in_specs=[pl.BlockSpec((kb, hc, f), lambda i, c: (i, c[0], 0))] * 3 + [pl.BlockSpec(memory_space=pl.ANY)],
            out_specs=[vm] * 4, scratch_shapes=[pltpu.SemaphoreType.DMA]),
        out_shape=[jax.ShapeDtypeStruct((hc, d, f), BF16)] * 3 + [jax.ShapeDtypeStruct((hc, f, d), BF16)],
        cost_estimate=pl.CostEstimate(flops=10**10, bytes_accessed=4 * d * hc * f * 2, transcendentals=0),
        compiler_params=pltpu.CompilerParams(vmem_limit_bytes=16 * 2**20))(core, wq, wk, wv, wo)


def layer_kernel(u_ref, v_ref, w_ref, q_ref, k_ref, vw_ref, o_ref, mine_ref, mate_ref, x_s):
    half, d = u_ref.shape
    hc = q_ref.shape[0]
    nb = 2 * half // 128
    for j, r_ref in enumerate((u_ref, v_ref)):
        for b in range(half // 128):
            uf = r_ref[b * 128:(b + 1) * 128].astype(F32)
            r = lax.rsqrt(jnp.mean(uf * uf, axis=-1, keepdims=True) + EPS)
            x_s[j * half + b * 128:j * half + (b + 1) * 128] = (uf * r * w_ref[...]).astype(BF16)
    keep = lax.broadcasted_iota(jnp.int32, (128, 128), 0) >= lax.broadcasted_iota(jnp.int32, (128, 128), 1)

    def heads(i):
        at = i * HS

        def proj(ref):
            wt = jnp.concatenate([ref[at + j] for j in range(HS)], axis=1)
            return jnp.dot(x_s[...], wt, preferred_element_type=F32).astype(BF16)

        q, k, v = proj(q_ref), proj(k_ref), proj(vw_ref)
        a = attn(q, k, v, nb, keep)
        return jnp.dot(a, o_ref[pl.ds(at, HS)].reshape(a.shape[1], d), preferred_element_type=F32)

    t = heads(0)
    mine_ref[...] = t[:half]
    mate_ref[...] = t[half:]

    def more(i, _):
        t = heads(i)
        mine_ref[...] += t[:half]
        mate_ref[...] += t[half:]
        return 0

    lax.fori_loop(1, hc // HS, more, 0)


def layer(u, v, w, wq, wk, wv, wo):
    m, d = u.shape
    hc, _, f = wq.shape
    vm = pl.BlockSpec(memory_space=pltpu.VMEM)
    return pl.pallas_call(
        layer_kernel, name="layer", in_specs=[vm] * 7, out_specs=[vm] * 2,
        scratch_shapes=[pltpu.VMEM((2 * m, d), BF16)],
        out_shape=[jax.ShapeDtypeStruct((m, d), F32)] * 2,
        cost_estimate=pl.CostEstimate(flops=2 * 2 * m * d * hc * f * 4 * 2, bytes_accessed=4 * d * hc * f * 2, transcendentals=0),
        compiler_params=pltpu.CompilerParams(vmem_limit_bytes=20 * 2**20))(u, v, w, wq, wk, wv, wo)


def solution(mesh):
    npp = mesh.shape['pp']
    nep = mesh.shape['ep']
    perm = [(i, (i + 1) % npp) for i in range(npp)]
    mate = [(i, i ^ 1) for i in range(nep)]
    across = [(i, i ^ 2) for i in range(nep)]
    tok = P(('data', 'pp'), None, 'ep', None, None)
    wsp = P('pp', None, None, None)

    def step(O, idx, slot, g, H, w, Wq, Wk, Wv, Wo):
        o = O[0]
        mb, ne, cap, d = o.shape
        cg = cap // nep
        o5 = o.reshape(mb, ne, nep, cg, d)
        e = lax.axis_index('ep')
        core = e % 2
        ix, sl, gt = (jnp.swapaxes(a[0][:, 0], 1, 2) for a in (idx, slot, g))

        def place(chip, reader):
            k = ix - chip * (2 * ne)
            ok = (sl >= 0) & (k >= 0) & (k < 2 * ne)
            k = jnp.where(reader == 0, k, (k + ne) % (2 * ne))
            return jnp.where(ok, k * cg + sl - e * cg, -1).astype(F32)

        here = place(e // 2, core)
        sent = jnp.concatenate([place(1 - e // 2, core), gt], axis=1)
        part0, *far, near = front(sent, jnp.concatenate([here, gt], axis=1), o5)
        part = [part0]
        for m in range(1, mb):
            part.append(lax.ppermute(far[m - 1], 'ep', across))
        cs = jnp.reshape(core, (1,)).astype(jnp.int32)
        h = H[0][:, 0]
        z = [None] * mb

        def finish(m, near):
            return (h[m].astype(F32) + near[m] + part[m]).astype(BF16)

        def start(u):
            mine, other = layer(u, lax.ppermute(u, 'ep', mate), w, *wt)
            return u, mine, lax.ppermute(other, 'ep', mate)

        def end(u, mine, other):
            return (u.astype(F32) + (mine + other).astype(BF16).astype(F32)).astype(BF16)

        y = finish(0, near)
        ws, y, near = lax.optimization_barrier(((Wq[0], Wk[0], Wv[0], Wo[0]), y, near))
        late = lax.ppermute(y, 'pp', perm)
        wt = turn(cs, *ws)
        wt, near = lax.optimization_barrier((wt, near))
        for m in range(1, mb):
            y = finish(m, near)
            late, y = lax.optimization_barrier((late, y))
            u = lax.ppermute(y, 'pp', perm)
            last = start(late)
            z[m - 1] = last
            mine, near = lax.optimization_barrier((last[1], near))
            z[m - 1] = (last[0], mine, last[2])
            late = u
        z[mb - 1] = start(late)
        z = [end(*q) for q in z]
        return jnp.stack(z).reshape(1, mb, 1, H.shape[3], d)

    return jax.shard_map(step, mesh=mesh,
                         in_specs=(tok, tok, tok, tok, tok, P('pp', None), wsp, wsp, wsp, wsp),
                         out_specs=tok, check_vma=False)
```

profile of v0, /device:TPU:0, one launch (start us, length us, event | category | flops | bytes accessed | tf_op | source)
XLA Modules:
  0.0 185.0 jit_solution(15532378616430024867)
XLA Ops:
  0.0 0.8 fusion.37
  0.8 1.4 pad_maximum_fusion
  2.2 33.2 %front.1 = (f32[128,1792]{1,0:T(8,128)}, f32[128,1792]{1,0:T(8,128)}, f32[128,1792]{1,0:T(8,128)}, f32[128,1792]{1,0:T(8,128)}, f32[128,1792]{1,0:T(8,128)}, /*i...) custom-call(f32[6,16,128]{2,1,0:T(8,128)} %get-tuple-element.114.sent_ref, f32[6,16,128]{2,1,0:T(8,128)} %get-tuple-element.113.here_ref, ...), custom_call_target="tpu_custom_call" | custom-call | flops 12683575296 | tf_op jit(solution)/shard_map/front/pallas_call | solution.py:107
  35.4 0.0 slice-start
  35.4 1.7 fusion.11
  37.2 1.6 collective-permute-start
  38.8 0.5 collective-permute-start.1
  39.3 15.5 %turn.1 = (bf16[16,1792,128]{2,1,0:T(8,128)(2,1)S(1)}, bf16[16,1792,128]{2,1,0:T(8,128)(2,1)S(1)}, bf16[16,1792,128]{2,1,0:T(8,128)(2,1)S(1)}, bf16[16,128,1792]{2,1,0:T(8,128)(2,1)S(1)}) custom-call(s32[1]{0:T(128)} %bitcast.21.c_ref, bf16[1792,32,128]{2,1,0:T(8,128)(2,1)} %bitcast.129, bf16[1792,32,128]{2,1,0:T(8,128)(2,1)} %bitcast.130, ...), custom_call_target="tpu_custom_call" | custom-call | flops 10000000000 | bytes 29360128 | tf_op jit(solution)/shard_map/turn/pallas_call | solution.py:159
  54.8 0.0 copy-start
  54.8 6.4 %collective-permute-done.1 = f32[128,1792]{1,0:T(8,128)S(1)} collective-permute-done((f32[128,1792]{1,0:T(8,128)S(1)}, f32[128,1792]{1,0:T(8,128)S(1)}, u32[]{:S(2)}, u32[]{:S(2)}) %collective-permute-start.1) | collective-permute-done | bytes 917536 | tf_op jit(solution)/shard_map/ppermute | solution.py:246
  61.1 0.2 fusion.9
  61.3 0.0 collective-permute-done.u_ref
  61.3 0.1 collective-permute-start.2
  61.4 0.6 collective-permute-start.5
  62.0 1.6 collective-permute-start.4
  63.5 0.0 collective-permute-done.2.v_ref
  63.6 11.0 %layer.6 = (f32[128,1792]{1,0:T(8,128)S(1)}, f32[128,1792]{1,0:T(8,128)S(1)}) custom-call(bf16[128,1792]{1,0:T(8,128)(2,1)S(1)} %collective-permute-done.u_ref, bf16[128,1792]{1,0:T(8,128)(2,1)S(1)} %collective-permute-done.2.v_ref, f32[1,1792]{1,0:T(1,128)S(1)} %copy-done, bf16[16,1792,128]{2,1,0:T(8,128)(2,1)S(1)} %get-tuple-element.73.q_ref, ...), custom_call_target="tpu_custom_call" | custom-call | flops 15032385536 | bytes 29360128 | tf_op jit(solution)/shard_map/layer/pallas_call | solution.py:209
  74.6 9.6 %collective-permute-done.5 = f32[128,1792]{1,0:T(8,128)S(1)} collective-permute-done((f32[128,1792]{1,0:T(8,128)S(1)}, f32[128,1792]{1,0:T(8,128)S(1)}, u32[]{:S(2)}, u32[]{:S(2)}) %collective-permute-start.5) | collective-permute-done | bytes 917536 | tf_op jit(solution)/shard_map/ppermute | solution.py:246
  84.2 0.1 fusion.7
  84.3 0.1 collective-permute-start.6
  84.4 0.6 collective-permute-start.9
  84.9 1.6 collective-permute-start.8
  86.5 0.0 collective-permute-done.6.v_ref
  86.5 11.0 %layer.7 = (f32[128,1792]{1,0:T(8,128)S(1)}, f32[128,1792]{1,0:T(8,128)S(1)}) custom-call(bf16[128,1792]{1,0:T(8,128)(2,1)S(1)} %collective-permute-done.4.u_ref, bf16[128,1792]{1,0:T(8,128)(2,1)S(1)} %collective-permute-done.6.v_ref, f32[1,1792]{1,0:T(1,128)S(1)} %copy-done, bf16[16,1792,128]{2,1,0:T(8,128)(2,1)S(1)} %get-tuple-element.73.q_ref, ...), custom_call_target="tpu_custom_call" | custom-call | flops 15032385536 | bytes 29360128 | tf_op jit(solution)/shard_map/layer/pallas_call | solution.py:209
  97.5 9.6 %collective-permute-done.9 = f32[128,1792]{1,0:T(8,128)S(1)} collective-permute-done((f32[128,1792]{1,0:T(8,128)S(1)}, f32[128,1792]{1,0:T(8,128)S(1)}, u32[]{:S(2)}, u32[]{:S(2)}) %collective-permute-start.9) | collective-permute-done | bytes 917536 | tf_op jit(solution)/shard_map/ppermute | solution.py:246
  107.1 0.1 fusion.5
  107.2 0.0 collective-permute-done.8.u_ref
  107.2 0.1 collective-permute-start.10
  107.3 0.6 collective-permute-start.13
  107.9 1.5 collective-permute-start.17
  109.4 0.0 collective-permute-start.3
  109.4 1.6 collective-permute-start.12
  111.0 0.0 collective-permute-done.10.v_ref
  111.0 0.2 collective-permute-start.7
  111.2 11.0 %layer.8 = (f32[128,1792]{1,0:T(8,128)S(1)}, f32[128,1792]{1,0:T(8,128)S(1)}) custom-call(bf16[128,1792]{1,0:T(8,128)(2,1)S(1)} %collective-permute-done.8.u_ref, bf16[128,1792]{1,0:T(8,128)(2,1)S(1)} %collective-permute-done.10.v_ref, f32[1,1792]{1,0:T(1,128)S(1)} %copy-done, bf16[16,1792,128]{2,1,0:T(8,128)(2,1)S(1)} %get-tuple-element.73.q_ref, ...), custom_call_target="tpu_custom_call" | custom-call | flops 15032385536 | bytes 29360128 | tf_op jit(solution)/shard_map/layer/pallas_call | solution.py:209
  122.2 8.7 %collective-permute-done.13 = f32[128,1792]{1,0:T(8,128)} collective-permute-done((f32[128,1792]{1,0:T(8,128)}, f32[128,1792]{1,0:T(8,128)}, u32[]{:S(2)}, u32[]{:S(2)}) %collective-permute-start.13) | collective-permute-done | bytes 917536 | tf_op jit(solution)/shard_map/ppermute | solution.py:246
  130.9 2.1 %fusion.3 = bf16[128,1792]{1,0:T(8,128)(2,1)} fusion(f32[128,1792]{1,0:T(8,128)} %collective-permute-done.13, f32[6,128,1792]{2,1,0:T(8,128)S(1)} %bitcast.134, bf16[1,6,1,128,1792]{4,3,2,1,0:T(8,128)(2,1)S(1)} %copy-done.1), kind=kLoop, calls=%fused_computation.5 | loop fusion | flops 917504 | bytes 2752512 | tf_op jit(solution)/shard_map/convert_element_type | solution.py:252
  133.0 0.0 collective-permute-done.12.u_ref
  133.0 1.6 collective-permute-start.16
  134.6 0.0 collective-permute-done.3
  134.6 0.5 collective-permute-start.11
  135.1 2.1 %fusion.13 = bf16[6,128,1792]{2,1,0:T(8,128)(2,1)} fusion(f32[128,1792]{1,0:T(8,128)S(1)} %get-tuple-element.78, f32[128,1792]{1,0:T(8,128)} %collective-permute-done.3, bf16[128,1792]{1,0:T(8,128)(2,1)S(1)} %collective-permute-done.u_ref), kind=kLoop, calls=%fused_computation.31 | loop fusion | flops 1376255 | bytes 2752512
  137.2 0.0 collective-permute-done.14.v_ref
  137.2 11.0 %layer.9 = (f32[128,1792]{1,0:T(8,128)S(1)}, f32[128,1792]{1,0:T(8,128)S(1)}) custom-call(bf16[128,1792]{1,0:T(8,128)(2,1)S(1)} %collective-permute-done.12.u_ref, bf16[128,1792]{1,0:T(8,128)(2,1)S(1)} %collective-permute-done.14.v_ref, f32[1,1792]{1,0:T(1,128)S(1)} %copy-done, bf16[16,1792,128]{2,1,0:T(8,128)(2,1)S(1)} %get-tuple-element.73.q_ref, ...), custom_call_target="tpu_custom_call" | custom-call | flops 15032385536 | bytes 29360128 | tf_op jit(solution)/shard_map/layer/pallas_call | solution.py:209
  148.3 1.8 collective-permute-done.17
  150.0 2.1 %fusion.1 = bf16[128,1792]{1,0:T(8,128)(2,1)} fusion(f32[128,1792]{1,0:T(8,128)} %collective-permute-done.17, f32[6,128,1792]{2,1,0:T(8,128)S(1)} %bitcast.134, bf16[1,6,1,128,1792]{4,3,2,1,0:T(8,128)(2,1)S(1)} %copy-done.1), kind=kLoop, calls=%fused_computation.2 | loop fusion | flops 917504 | bytes 2752512 | tf_op jit(solution)/shard_map/convert_element_type | solution.py:252
  152.2 0.0 collective-permute-done.16.u_ref
  152.2 1.6 collective-permute-start.20
  153.8 0.5 collective-permute-start.15
  154.3 2.1 %fusion.15 = bf16[6,128,1792]{2,1,0:T(8,128)(2,1)} fusion(bf16[6,128,1792]{2,1,0:T(8,128)(2,1)} %fusion.13, f32[128,1792]{1,0:T(8,128)S(1)} %get-tuple-element.85, f32[128,1792]{1,0:T(8,128)} %collective-permute-done.7, bf16[128,1792]{1,0:T(8,128)(2,1)S(1)} %collective-permute-done.4.u_ref), kind=kLoop, calls=%fused_computation.33 | loop fusion | flops 1376256 | bytes 2752512
  156.4 0.0 collective-permute-done.18.v_ref
  156.4 11.0 %layer.10 = (f32[128,1792]{1,0:T(8,128)S(1)}, f32[128,1792]{1,0:T(8,128)S(1)}) custom-call(bf16[128,1792]{1,0:T(8,128)(2,1)S(1)} %collective-permute-done.16.u_ref, bf16[128,1792]{1,0:T(8,128)(2,1)S(1)} %collective-permute-done.18.v_ref, f32[1,1792]{1,0:T(1,128)S(1)} %copy-done, bf16[16,1792,128]{2,1,0:T(8,128)(2,1)S(1)} %get-tuple-element.73.q_ref, ...), custom_call_target="tpu_custom_call" | custom-call | flops 15032385536 | bytes 29360128 | tf_op jit(solution)/shard_map/layer/pallas_call | solution.py:209
  167.4 0.1 collective-permute-start.19
  167.5 0.0 collective-permute-done.20.u_ref
  167.5 0.5 collective-permute-start.21
  168.0 0.0 collective-permute-done.11
  168.0 2.1 %fusion.17 = bf16[6,128,1792]{2,1,0:T(8,128)(2,1)} fusion(bf16[6,128,1792]{2,1,0:T(8,128)(2,1)} %fusion.15, f32[128,1792]{1,0:T(8,128)S(1)} %get-tuple-element.92, f32[128,1792]{1,0:T(8,128)} %collective-permute-done.11, bf16[128,1792]{1,0:T(8,128)(2,1)S(1)} %collective-permute-done.8.u_ref), kind=kLoop, calls=%fused_computation.35 | loop fusion | flops 1376256 | bytes 2752512
  170.1 0.5 collective-permute-done.21.v_ref
  170.6 11.0 %layer.11 = (f32[128,1792]{1,0:T(8,128)S(1)}, f32[128,1792]{1,0:T(8,128)S(1)}) custom-call(bf16[128,1792]{1,0:T(8,128)(2,1)S(1)} %collective-permute-done.20.u_ref, bf16[128,1792]{1,0:T(8,128)(2,1)S(1)} %collective-permute-done.21.v_ref, f32[1,1792]{1,0:T(1,128)S(1)} %copy-done, bf16[16,1792,128]{2,1,0:T(8,128)(2,1)S(1)} %get-tuple-element.73.q_ref, ...), custom_call_target="tpu_custom_call" | custom-call | flops 15032385536 | bytes 29360128 | tf_op jit(solution)/shard_map/layer/pallas_call | solution.py:209
  181.6 0.2 collective-permute-start.22
  181.8 0.9 fusion.19
  182.7 0.9 fusion.21
  183.6 0.6 collective-permute-done.22
  184.2 0.9 fusion.23
  (19 shorter events, 0.0 us)
Async XLA Ops:
  2.2 33.2 %copy-start.1 = (bf16[1,6,1,128,1792]{4,3,2,1,0:T(8,128)(2,1)S(1)}, bf16[1,6,1,128,1792]{4,3,2,1,0:T(8,128)(2,1)}, u32[]{:S(2)}) copy-start(bf16[1,6,1,128,1792]{4,3,2,1,0:T(8,128)(2,1)} %param.14) | copy-start | bytes 8257540
  35.4 3.4 %copy-start.4 = (f32[128,1792]{1,0:T(8,128)S(1)}, f32[128,1792]{1,0:T(8,128)}, u32[]{:S(2)}) copy-start(f32[128,1792]{1,0:T(8,128)} %get-tuple-element.71) | copy-start | bytes 2752516
  35.4 25.7 %slice-start = ((s8[5505024]{0:T(1024)(128)(4,1)}), s8[4194304]{0:T(1024)(128)(4,1)S(1)}, s32[]{:S(2)}) async-start(s8[5505024]{0:T(1024)(128)(4,1)} %bitcast.133), calls=%async_computation | async-start | bytes 8388608
  37.2 24.2 %collective-permute-start = (bf16[128,1792]{1,0:T(8,128)(2,1)S(1)}, bf16[128,1792]{1,0:T(8,128)(2,1)S(1)}, u32[]{:S(2)}, u32[]{:S(2)}) collective-permute-start(bf16[128,1792]{1,0:T(8,128)(2,1)S(1)} %fusion.11), channel_id=1, source_target_pairs={{0,4},{4,8},{8,12},{12,0},{1,5},{5,9},{9,13},{13,1},{2,6},{6,10},{... | collective-permute-start | bytes 1376264 | tf_op jit(solution)/shard_map/ppermute | solution.py:263
  38.8 22.4 %collective-permute-start.1 = (f32[128,1792]{1,0:T(8,128)S(1)}, f32[128,1792]{1,0:T(8,128)S(1)}, u32[]{:S(2)}, u32[]{:S(2)}) collective-permute-start(f32[128,1792]{1,0:T(8,128)S(1)} %copy-done.4), channel_id=1, source_target_pairs={{0,2},{1,3},{2,0},{3,1},{4,6},{5,7},{6,4},{7,5},{8,10},{9,11},{10,... | collective-permute-start | bytes 2752520 | tf_op jit(solution)/shard_map/ppermute | solution.py:246
  39.3 21.8 %slice-start.1 = ((s8[5505024]{0:T(1024)(128)(4,1)}), s8[1310720]{0:T(1024)(128)(4,1)S(1)}, s32[]{:S(2)}) async-start(s8[5505024]{0:T(1024)(128)(4,1)} %bitcast.133), calls=%async_computation.1 | async-start | bytes 2621440
  54.8 6.6 %copy-start.3 = (f32[128,1792]{1,0:T(8,128)S(1)}, f32[128,1792]{1,0:T(8,128)}, u32[]{:S(2)}) copy-start(f32[128,1792]{1,0:T(8,128)} %get-tuple-element.82) | copy-start | bytes 2752516
  54.8 8.8 %copy-start = (f32[1,1792]{1,0:T(1,128)S(1)}, f32[1,1792]{1,0:T(1,128)}, u32[]{:S(2)}) copy-start(f32[1,1792]{1,0:T(1,128)} %w_ref.11) | copy-start | bytes 21508
  61.3 2.2 %collective-permute-start.2 = (bf16[128,1792]{1,0:T(8,128)(2,1)S(1)}, bf16[128,1792]{1,0:T(8,128)(2,1)S(1)}, u32[]{:S(2)}, u32[]{:S(2)}) collective-permute-start(bf16[128,1792]{1,0:T(8,128)(2,1)S(1)} %collective-permute-done.u_ref), channel_id=1, source_target_pairs={{0,1},{1,0},{2,3},{3,2},{4,5},{5,4},{6,7},{7,6},{8,9},{9,8},{10,11... | collective-permute-start | bytes 1376264 | tf_op jit(solution)/shard_map/ppermute | solution.py:255
  61.4 22.7 %collective-permute-start.5 = (f32[128,1792]{1,0:T(8,128)S(1)}, f32[128,1792]{1,0:T(8,128)S(1)}, u32[]{:S(2)}, u32[]{:S(2)}) collective-permute-start(f32[128,1792]{1,0:T(8,128)S(1)} %copy-done.3), channel_id=1, source_target_pairs={{0,2},{1,3},{2,0},{3,1},{4,6},{5,7},{6,4},{7,5},{8,10},{9,11},{10,... | collective-permute-start | bytes 2752520 | tf_op jit(solution)/shard_map/ppermute | solution.py:246
  62.0 22.3 %collective-permute-start.4 = (bf16[128,1792]{1,0:T(8,128)(2,1)S(1)}, bf16[128,1792]{1,0:T(8,128)(2,1)S(1)}, u32[]{:S(2)}, u32[]{:S(2)}) collective-permute-start(bf16[128,1792]{1,0:T(8,128)(2,1)S(1)} %fusion.9), channel_id=1, source_target_pairs={{0,4},{4,8},{8,12},{12,0},{1,5},{5,9},{9,13},{13,1},{2,6},{6,10},{... | collective-permute-start | bytes 1376264 | tf_op jit(solution)/shard_map/ppermute | solution.py:269
  74.6 9.8 %copy-start.2 = (f32[128,1792]{1,0:T(8,128)S(1)}, f32[128,1792]{1,0:T(8,128)}, u32[]{:S(2)}) copy-start(f32[128,1792]{1,0:T(8,128)} %get-tuple-element.89) | copy-start | bytes 2752516
  84.3 2.2 %collective-permute-start.6 = (bf16[128,1792]{1,0:T(8,128)(2,1)S(1)}, bf16[128,1792]{1,0:T(8,128)(2,1)S(1)}, u32[]{:S(2)}, u32[]{:S(2)}) collective-permute-start(bf16[128,1792]{1,0:T(8,128)(2,1)S(1)} %collective-permute-done.4.u_ref), channel_id=1, source_target_pairs={{0,1},{1,0},{2,3},{3,2},{4,5},{5,4},{6,7},{7,6},{8,9},{9,8},{10,11... | collective-permute-start | bytes 1376264 | tf_op jit(solution)/shard_map/ppermute | solution.py:255
  84.4 22.7 %collective-permute-start.9 = (f32[128,1792]{1,0:T(8,128)S(1)}, f32[128,1792]{1,0:T(8,128)S(1)}, u32[]{:S(2)}, u32[]{:S(2)}) collective-permute-start(f32[128,1792]{1,0:T(8,128)S(1)} %copy-done.2), channel_id=1, source_target_pairs={{0,2},{1,3},{2,0},{3,1},{4,6},{5,7},{6,4},{7,5},{8,10},{9,11},{10,... | collective-permute-start | bytes 2752520 | tf_op jit(solution)/shard_map/ppermute | solution.py:246
  84.9 22.3 %collective-permute-start.8 = (bf16[128,1792]{1,0:T(8,128)(2,1)S(1)}, bf16[128,1792]{1,0:T(8,128)(2,1)S(1)}, u32[]{:S(2)}, u32[]{:S(2)}) collective-permute-start(bf16[128,1792]{1,0:T(8,128)(2,1)S(1)} %fusion.7), channel_id=1, source_target_pairs={{0,4},{4,8},{8,12},{12,0},{1,5},{5,9},{9,13},{13,1},{2,6},{6,10},{... | collective-permute-start | bytes 1376264 | tf_op jit(solution)/shard_map/ppermute | solution.py:269
  107.2 3.8 %collective-permute-start.10 = (bf16[128,1792]{1,0:T(8,128)(2,1)S(1)}, bf16[128,1792]{1,0:T(8,128)(2,1)S(1)}, u32[]{:S(2)}, u32[]{:S(2)}) collective-permute-start(bf16[128,1792]{1,0:T(8,128)(2,1)S(1)} %collective-permute-done.8.u_ref), channel_id=1, source_target_pairs={{0,1},{1,0},{2,3},{3,2},{4,5},{5,4},{6,7},{7,6},{8,9},{9,8},{10,11... | collective-permute-start | bytes 1376264 | tf_op jit(solution)/shard_map/ppermute | solution.py:255
  107.3 23.6 %collective-permute-start.13 = (f32[128,1792]{1,0:T(8,128)}, f32[128,1792]{1,0:T(8,128)}, u32[]{:S(2)}, u32[]{:S(2)}) collective-permute-start(f32[128,1792]{1,0:T(8,128)} %get-tuple-element.96), channel_id=1, source_target_pairs={{0,2},{1,3},{2,0},{3,1},{4,6},{5,7},{6,4},{7,5},{8,10},{9,11},{10,... | collective-permute-start | bytes 2752520 | tf_op jit(solution)/shard_map/ppermute | solution.py:246
  107.9 42.2 %collective-permute-start.17 = (f32[128,1792]{1,0:T(8,128)}, f32[128,1792]{1,0:T(8,128)}, u32[]{:S(2)}, u32[]{:S(2)}) collective-permute-start(f32[128,1792]{1,0:T(8,128)} %get-tuple-element.103), channel_id=1, source_target_pairs={{0,2},{1,3},{2,0},{3,1},{4,6},{5,7},{6,4},{7,5},{8,10},{9,11},{10,... | collective-permute-start | bytes 2752520 | tf_op jit(solution)/shard_map/ppermute | solution.py:246
  109.4 25.2 %collective-permute-start.3 = (f32[128,1792]{1,0:T(8,128)S(1)}, f32[128,1792]{1,0:T(8,128)}, u32[]{:S(2)}, u32[]{:S(2)}) collective-permute-start(f32[128,1792]{1,0:T(8,128)S(1)} %get-tuple-element.79), channel_id=1, source_target_pairs={{0,1},{1,0},{2,3},{3,2},{4,5},{5,4},{6,7},{7,6},{8,9},{9,8},{10,11... | collective-permute-start | bytes 2752520 | tf_op jit(solution)/shard_map/ppermute | solution.py:256
  109.4 23.6 %collective-permute-start.12 = (bf16[128,1792]{1,0:T(8,128)(2,1)S(1)}, bf16[128,1792]{1,0:T(8,128)(2,1)S(1)}, u32[]{:S(2)}, u32[]{:S(2)}) collective-permute-start(bf16[128,1792]{1,0:T(8,128)(2,1)S(1)} %fusion.5), channel_id=1, source_target_pairs={{0,4},{4,8},{8,12},{12,0},{1,5},{5,9},{9,13},{13,1},{2,6},{6,10},{... | collective-permute-start | bytes 1376264 | tf_op jit(solution)/shard_map/ppermute | solution.py:269
  111.0 43.3 %collective-permute-start.7 = (f32[128,1792]{1,0:T(8,128)S(1)}, f32[128,1792]{1,0:T(8,128)}, u32[]{:S(2)}, u32[]{:S(2)}) collective-permute-start(f32[128,1792]{1,0:T(8,128)S(1)} %get-tuple-element.86), channel_id=1, source_target_pairs={{0,1},{1,0},{2,3},{3,2},{4,5},{5,4},{6,7},{7,6},{8,9},{9,8},{10,11... | collective-permute-start | bytes 2752520 | tf_op jit(solution)/shard_map/ppermute | solution.py:256
  133.0 19.1 %collective-permute-start.16 = (bf16[128,1792]{1,0:T(8,128)(2,1)}, bf16[128,1792]{1,0:T(8,128)(2,1)S(1)}, u32[]{:S(2)}, u32[]{:S(2)}) collective-permute-start(bf16[128,1792]{1,0:T(8,128)(2,1)} %fusion.3), channel_id=1, source_target_pairs={{0,4},{4,8},{8,12},{12,0},{1,5},{5,9},{9,13},{13,1},{2,6},{6,10},{... | collective-permute-start | bytes 1376264 | tf_op jit(solution)/shard_map/ppermute | solution.py:269
  134.6 2.6 %collective-permute-start.14 = (bf16[128,1792]{1,0:T(8,128)(2,1)S(1)}, bf16[128,1792]{1,0:T(8,128)(2,1)S(1)}, u32[]{:S(2)}, u32[]{:S(2)}) collective-permute-start(bf16[128,1792]{1,0:T(8,128)(2,1)S(1)} %collective-permute-done.12.u_ref), channel_id=1, source_target_pairs={{0,1},{1,0},{2,3},{3,2},{4,5},{5,4},{6,7},{7,6},{8,9},{9,8},{10,11... | collective-permute-start | bytes 1376264 | tf_op jit(solution)/shard_map/ppermute | solution.py:255
  134.6 33.4 %collective-permute-start.11 = (f32[128,1792]{1,0:T(8,128)S(1)}, f32[128,1792]{1,0:T(8,128)}, u32[]{:S(2)}, u32[]{:S(2)}) collective-permute-start(f32[128,1792]{1,0:T(8,128)S(1)} %get-tuple-element.93), channel_id=1, source_target_pairs={{0,1},{1,0},{2,3},{3,2},{4,5},{5,4},{6,7},{7,6},{8,9},{9,8},{10,11... | collective-permute-start | bytes 2752520 | tf_op jit(solution)/shard_map/ppermute | solution.py:256
  152.2 15.3 %collective-permute-start.20 = (bf16[128,1792]{1,0:T(8,128)(2,1)}, bf16[128,1792]{1,0:T(8,128)(2,1)S(1)}, u32[]{:S(2)}, u32[]{:S(2)}) collective-permute-start(bf16[128,1792]{1,0:T(8,128)(2,1)} %fusion.1), channel_id=1, source_target_pairs={{0,4},{4,8},{8,12},{12,0},{1,5},{5,9},{9,13},{13,1},{2,6},{6,10},{... | collective-permute-start | bytes 1376264 | tf_op jit(solution)/shard_map/ppermute | solution.py:269
  153.8 2.6 %collective-permute-start.18 = (bf16[128,1792]{1,0:T(8,128)(2,1)S(1)}, bf16[128,1792]{1,0:T(8,128)(2,1)S(1)}, u32[]{:S(2)}, u32[]{:S(2)}) collective-permute-start(bf16[128,1792]{1,0:T(8,128)(2,1)S(1)} %collective-permute-done.16.u_ref), channel_id=1, source_target_pairs={{0,1},{1,0},{2,3},{3,2},{4,5},{5,4},{6,7},{7,6},{8,9},{9,8},{10,11... | collective-permute-start | bytes 1376264 | tf_op jit(solution)/shard_map/ppermute | solution.py:255
  153.8 28.1 %collective-permute-start.15 = (f32[128,1792]{1,0:T(8,128)S(1)}, f32[128,1792]{1,0:T(8,128)S(1)}, u32[]{:S(2)}, u32[]{:S(2)}) collective-permute-start(f32[128,1792]{1,0:T(8,128)S(1)} %get-tuple-element.100), channel_id=1, source_target_pairs={{0,1},{1,0},{2,3},{3,2},{4,5},{5,4},{6,7},{7,6},{8,9},{9,8},{10,11... | collective-permute-start | bytes 2752520 | tf_op jit(solution)/shard_map/ppermute | solution.py:256
  167.4 15.3 %collective-permute-start.19 = (f32[128,1792]{1,0:T(8,128)S(1)}, f32[128,1792]{1,0:T(8,128)S(1)}, u32[]{:S(2)}, u32[]{:S(2)}) collective-permute-start(f32[128,1792]{1,0:T(8,128)S(1)} %get-tuple-element.107), channel_id=1, source_target_pairs={{0,1},{1,0},{2,3},{3,2},{4,5},{5,4},{6,7},{7,6},{8,9},{9,8},{10,11... | collective-permute-start | bytes 2752520 | tf_op jit(solution)/shard_map/ppermute | solution.py:256
  167.5 3.1 %collective-permute-start.21 = (bf16[128,1792]{1,0:T(8,128)(2,1)S(1)}, bf16[128,1792]{1,0:T(8,128)(2,1)S(1)}, u32[]{:S(2)}, u32[]{:S(2)}) collective-permute-start(bf16[128,1792]{1,0:T(8,128)(2,1)S(1)} %collective-permute-done.20.u_ref), channel_id=1, source_target_pairs={{0,1},{1,0},{2,3},{3,2},{4,5},{5,4},{6,7},{7,6},{8,9},{9,8},{10,11... | collective-permute-start | bytes 1376264 | tf_op jit(solution)/shard_map/ppermute | solution.py:255
  181.6 2.5 %collective-permute-start.22 = (f32[128,1792]{1,0:T(8,128)S(1)}, f32[128,1792]{1,0:T(8,128)S(1)}, u32[]{:S(2)}, u32[]{:S(2)}) collective-permute-start(f32[128,1792]{1,0:T(8,128)S(1)} %get-tuple-element.110), channel_id=1, source_target_pairs={{0,1},{1,0},{2,3},{3,2},{4,5},{5,4},{6,7},{7,6},{8,9},{9,8},{10,11... | collective-permute-start | bytes 2752520 | tf_op jit(solution)/shard_map/ppermute | solution.py:256
where the time goes:
time: 186 us; the launch traced here: 185 us
  Pallas kernels  115 us (62%)
  waiting for transfers between devices  37.1 us (20%)
  other arithmetic  17.5 us (9%)
  starting transfers between devices  15.5 us (8%)
    pallas_call x6, Pallas kernels, layer(): pl.pallas_call(layer_kernel, name='layer', in_specs=[vm] * 7, out_specs=[...  66.1 us
    ppermute x5, waiting for transfers between devices, step(): part.append(lax.ppermute(far[m - 1], 'ep', across))  36 us
    pallas_call x1, Pallas kernels, front(): pl.pallas_call(front_kernel, name='front', in_specs=[vm, vm, any_], out_s...  33.2 us
    pallas_call x1, Pallas kernels, turn(): pl.pallas_call(turn_kernel, name='turn', grid_spec=pltpu.PrefetchScalarGr...  15.5 us
    unnamed x6, other arithmetic  8.1 us
    ppermute x5, starting transfers between devices, step(): u = lax.ppermute(y, 'pp', perm)  7.88 us
    convert_element_type x6, other arithmetic, finish(): return (h[m].astype(F32) + near[m] + part[m]).astype(BF16)  6.37 us
    ppermute x5, starting transfers between devices, step(): part.append(lax.ppermute(far[m - 1], 'ep', across))  3.74 us
  transfers between devices with their start and end apart: 23, of which 7 were waited for; matrix products, arithmetic and copies ran while one was open for 7% of the time, Pallas kernels for 44%

commit v1 on v0

--- a/solution.py
+++ b/solution.py
@@ -12,6 +12,7 @@
 NT = (((1,), (1,)), ((), ()))
 VMEM_LIMIT = 60 * 2**20
 HS = 4
+IN_FRONT = 2
 
 
 def gate_terms(pos, gate, g_s, slot):
@@ -31,23 +32,33 @@
     g_s[slot, 2 * t:3 * t] = (rest - mid.astype(F32)).astype(BF16)
 
 
-def front_kernel(sent_ref, here_ref, o_ref, part_ref, *rest):
-    n_mb = sent_ref.shape[0]
-    far_refs, (near_ref, pg, rows, sums, g_s, own_sem, row_send, row_recv, pg_sem, y_sem, out_sem) = rest[:n_mb - 1], rest[n_mb - 1:]
-    n_ep = o_ref.shape[2]
-    d = o_ref.shape[-1]
+def place(ix, sl, chip, core, e, ne, cg):
+    k = ix - chip * (2 * ne)
+    ok = (sl >= 0) & (k >= 0) & (k < 2 * ne)
+    k = jnp.where(k >= ne, k - ne, k + ne) * core + k * (1 - core)
+    return jnp.where(ok, k * cg + sl - e * cg, -1).astype(F32)
+
+
+def front_kernel(ix_ref, sl_ref, gt_ref, o_ref, *rest):
+    n_mb, ne, n_ep, cg, d = o_ref.shape
+    in_refs, far_refs = rest[:IN_FRONT], rest[IN_FRONT:n_mb]
+    near_ref, sent, pg, rows, sums, g_s, own_sem, row_send, row_recv, pg_sem, y_send, y_recv, out_sem = rest[n_mb:]
     t = g_s.shape[1] // 3
     e = lax.axis_index('ep')
-    mate = e + 1 - 2 * lax.rem(e, 2)
+    core = lax.rem(e, 2)
+    chip = e // 2
+    mate = e + 1 - 2 * core
     across = lax.rem(e + 2, n_ep)
     mate_across = lax.rem(mate + 2, n_ep)
 
+    sent[:, :8] = place(ix_ref[...], sl_ref[...], 1 - chip, core, e, ne, cg)
+    sent[:, 8:] = gt_ref[...]
     barrier = pltpu.get_barrier_semaphore()
     for dev in (mate, across):
         pl.semaphore_signal(barrier, inc=1, device_id={'ep': dev}, device_id_type=pl.DeviceIdType.MESH)
     pl.semaphore_wait(barrier, 2)
 
-    gates = pltpu.make_async_remote_copy(sent_ref, pg.at[pl.ds(0, n_mb)], pg_sem.at[0], pg_sem.at[1],
+    gates = pltpu.make_async_remote_copy(sent, pg.at[pl.ds(0, n_mb)], pg_sem.at[0], pg_sem.at[1],
                                          device_id={'ep': across}, device_id_type=pl.DeviceIdType.MESH)
     gates.start()
     own, got = [], []
@@ -59,7 +70,8 @@
         own.append(pltpu.make_async_copy(o_ref.at[m, :, mine], rows.at[i, 0], own_sem.at[i]))
         got[i].start()
         own[i].start()
-    pg[n_mb:] = here_ref[...]
+    pg[n_mb:, :8] = place(ix_ref[...], sl_ref[...], chip, core, e, ne, cg)
+    pg[n_mb:, 8:] = gt_ref[...]
     gates.wait()
 
     def wait_rows(i):
@@ -81,38 +93,39 @@
         return 0
 
     gates_of(0)
-    one(0, 0)
-    first = pltpu.make_async_remote_copy(sums.at[0], part_ref, y_sem.at[0], y_sem.at[1],
-                                         device_id={'ep': across}, device_id_type=pl.DeviceIdType.MESH)
-    first.start()
-    lax.fori_loop(1, n_mb, one, 0)
-    outs = [pltpu.make_async_copy(sums.at[m], far_refs[m - 1], out_sem.at[m]) for m in range(1, n_mb)]
+    first = []
+    for i in range(IN_FRONT):
+        one(i, 0)
+        first.append(pltpu.make_async_remote_copy(sums.at[i], in_refs[i], y_send.at[i], y_recv.at[i],
+                                                  device_id={'ep': across}, device_id_type=pl.DeviceIdType.MESH))
+        first[i].start()
+    lax.fori_loop(IN_FRONT, n_mb, one, 0)
+    outs = [pltpu.make_async_copy(sums.at[m], far_refs[m - IN_FRONT], out_sem.at[m]) for m in range(IN_FRONT, n_mb)]
     for c in outs:
         c.start()
     lax.fori_loop(n_mb, 2 * n_mb, one, 0)
     near = pltpu.make_async_copy(sums.at[pl.ds(n_mb, n_mb)], near_ref, out_sem.at[0])
     near.start()
-    for c in outs + [near]:
+    for c in outs + [near] + first:
         c.wait()
-    first.wait()
-
-
-def front(sent, here, o5):
+
+
+def front(ix, sl, gt, o5):
     mb, ne, _, cg, d = o5.shape
-    t = sent.shape[2]
+    t = ix.shape[2]
     one = jax.ShapeDtypeStruct((t, d), F32)
     any_ = pl.BlockSpec(memory_space=pl.ANY)
     vm = pl.BlockSpec(memory_space=pltpu.VMEM)
     dma = pltpu.SemaphoreType.DMA
     return pl.pallas_call(
         front_kernel, name="front",
-        in_specs=[vm, vm, any_], out_specs=[any_] * (mb + 1),
+        in_specs=[vm, vm, vm, any_], out_specs=[any_] * (mb + 1),
         out_shape=[one] * mb + [jax.ShapeDtypeStruct((mb, t, d), F32)],
-        scratch_shapes=[pltpu.VMEM((2 * mb,) + sent.shape[1:], F32), pltpu.VMEM((2 * mb, 2, ne, cg, d), BF16),
+        scratch_shapes=[pltpu.VMEM((mb, 16, t), F32), pltpu.VMEM((2 * mb, 16, t), F32), pltpu.VMEM((2 * mb, 2, ne, cg, d), BF16),
                         pltpu.VMEM((2 * mb, t, d), F32), pltpu.VMEM((2, 3 * t, 2 * ne * cg), BF16),
-                        dma((2 * mb,)), dma((2 * mb,)), dma((2 * mb,)), dma((2,)), dma((2,)), dma((mb,))],
+                        dma((2 * mb,)), dma((2 * mb,)), dma((2 * mb,)), dma((2,)), dma((IN_FRONT,)), dma((IN_FRONT,)), dma((mb,))],
         cost_estimate=pl.CostEstimate(flops=2 * 3 * t * 2 * ne * cg * d * 2 * mb, bytes_accessed=0, transcendentals=0),
-        compiler_params=pltpu.CompilerParams(vmem_limit_bytes=VMEM_LIMIT, collective_id=0, has_side_effects=True))(sent, here, o5)
+        compiler_params=pltpu.CompilerParams(vmem_limit_bytes=VMEM_LIMIT, collective_id=0, has_side_effects=True))(ix, sl, gt, o5)
 
 
 def attn(q, k, v, nb, keep):
@@ -189,9 +202,8 @@
         a = attn(q, k, v, nb, keep)
         return jnp.dot(a, o_ref[pl.ds(at, HS)].reshape(a.shape[1], d), preferred_element_type=F32)
 
-    t = heads(0)
-    mine_ref[...] = t[:half]
-    mate_ref[...] = t[half:]
+    mine_ref[...] = jnp.zeros_like(mine_ref)
+    mate_ref[...] = jnp.zeros_like(mate_ref)
 
     def more(i, _):
         t = heads(i)
@@ -199,7 +211,7 @@
         mate_ref[...] += t[half:]
         return 0
 
-    lax.fori_loop(1, hc // HS, more, 0)
+    lax.fori_loop(0, hc // HS, more, 0)
 
 
 def layer(u, v, w, wq, wk, wv, wo):
@@ -211,7 +223,7 @@
         scratch_shapes=[pltpu.VMEM((2 * m, d), BF16)],
         out_shape=[jax.ShapeDtypeStruct((m, d), F32)] * 2,
         cost_estimate=pl.CostEstimate(flops=2 * 2 * m * d * hc * f * 4 * 2, bytes_accessed=4 * d * hc * f * 2, transcendentals=0),
-        compiler_params=pltpu.CompilerParams(vmem_limit_bytes=20 * 2**20))(u, v, w, wq, wk, wv, wo)
+        compiler_params=pltpu.CompilerParams(vmem_limit_bytes=12 * 2**20))(u, v, w, wq, wk, wv, wo)
 
 
 def solution(mesh):
@@ -232,18 +244,9 @@
         core = e % 2
         ix, sl, gt = (jnp.swapaxes(a[0][:, 0], 1, 2) for a in (idx, slot, g))
 
-        def place(chip, reader):
-            k = ix - chip * (2 * ne)
-            ok = (sl >= 0) & (k >= 0) & (k < 2 * ne)
-            k = jnp.where(reader == 0, k, (k + ne) % (2 * ne))
-            return jnp.where(ok, k * cg + sl - e * cg, -1).astype(F32)
-
-        here = place(e // 2, core)
-        sent = jnp.concatenate([place(1 - e // 2, core), gt], axis=1)
-        part0, *far, near = front(sent, jnp.concatenate([here, gt], axis=1), o5)
-        part = [part0]
-        for m in range(1, mb):
-            part.append(lax.ppermute(far[m - 1], 'ep', across))
+        *part, near = front(ix, sl, gt, o5)
+        for m in range(IN_FRONT, mb):
+            part[m] = lax.ppermute(part[m], 'ep', across)
         cs = jnp.reshape(core, (1,)).astype(jnp.int32)
         h = H[0][:, 0]
         z = [None] * mb
@@ -258,22 +261,26 @@
         def end(u, mine, other):
             return (u.astype(F32) + (mine + other).astype(BF16).astype(F32)).astype(BF16)
 
-        y = finish(0, near)
+        y = [finish(m, near) for m in range(IN_FRONT)]
         ws, y, near = lax.optimization_barrier(((Wq[0], Wk[0], Wv[0], Wo[0]), y, near))
-        late = lax.ppermute(y, 'pp', perm)
+        u = [lax.ppermute(x, 'pp', perm) for x in y]
         wt = turn(cs, *ws)
         wt, near = lax.optimization_barrier((wt, near))
-        for m in range(1, mb):
-            y = finish(m, near)
-            late, y = lax.optimization_barrier((late, y))
-            u = lax.ppermute(y, 'pp', perm)
-            last = start(late)
-            z[m - 1] = last
-            mine, near = lax.optimization_barrier((last[1], near))
-            z[m - 1] = (last[0], mine, last[2])
-            late = u
-        z[mb - 1] = start(late)
-        z = [end(*q) for q in z]
+        for m in range(IN_FRONT, mb + IN_FRONT):
+            k = m - IN_FRONT
+            late = u[k]
+            if m < mb:
+                y = finish(m, near)
+                late, y = lax.optimization_barrier((late, y))
+                u.append(lax.ppermute(y, 'pp', perm))
+            z[k] = start(late)
+            mine, near = lax.optimization_barrier((z[k][1], near))
+            z[k] = (z[k][0], mine, z[k][2])
+            if k > 0:
+                prev, mine = lax.optimization_barrier((z[k - 1], mine))
+                z[k - 1] = end(*prev)
+                z[k] = (z[k][0], mine, z[k][2])
+        z[mb - 1] = end(*z[mb - 1])
         return jnp.stack(z).reshape(1, mb, 1, H.shape[3], d)
 
     return jax.shard_map(step, mesh=mesh,

time: 186 us -> 196 us (1.054)
  Pallas kernels: 115 us -> 134 us
  other arithmetic: 17.5 us -> 6.89 us
  waiting for transfers between devices: 37.1 us -> 34.8 us
  starting transfers between devices: 15.5 us -> 17.8 us
    pallas_call x1, Pallas kernels: 33.2 us -> 49.6 us  [front(): pl.pallas_call(front_kernel, name='front', in_specs=[vm, vm, vm, any_], o...]
    unnamed x6 -> x5, other arithmetic: 8.1 us -> 0.6 us
    ppermute x11 -> x10, waiting for transfers between devices: 36 us -> 29.4 us  [the longest x4 29.4 us: step(): part[m] = lax.ppermute(part[m], 'ep', across)]
    ppermute x6, waiting for transfers between devices: 0.5 us -> 3.65 us  [start(): mine, other = layer(u, lax.ppermute(u, 'ep', mate), w, *wt)]
    pallas_call x6, Pallas kernels: 66.1 us -> 68.8 us  [layer(): pl.pallas_call(layer_kernel, name='layer', in_specs=[vm] * 7, out_specs=[...]
    ppermute x11 -> x10, starting transfers between devices: 13.2 us -> 15.8 us  [the longest x4 6.88 us: step(): part[m] = lax.ppermute(part[m], 'ep', across)]
    convert_element_type x6 -> x5, other arithmetic: 6.37 us -> 6.19 us  [finish(): return (h[m].astype(F32) + near[m] + part[m]).astype(BF16)]
  transfers between devices with their start and end apart: 23 -> 22, of which waited for: 7 -> 7; matrix products, arithmetic and copies ran while one was open for 7% -> 2% of each run, Pallas kernels for 44% -> 43%
where the time goes in v1:
time: 196 us; the launch traced here: 195 us
  Pallas kernels  134 us (68%)
  waiting for transfers between devices  34.8 us (18%)
  starting transfers between devices  17.8 us (9%)
  other arithmetic  6.89 us (4%)
    pallas_call x6, Pallas kernels, layer(): pl.pallas_call(layer_kernel, name='layer', in_specs=[vm] * 7, out_specs=[...  68.8 us
    pallas_call x1, Pallas kernels, front(): pl.pallas_call(front_kernel, name='front', in_specs=[vm, vm, vm, any_], o...  49.6 us
    ppermute x4, waiting for transfers between devices, step(): part[m] = lax.ppermute(part[m], 'ep', across)  29.4 us
    pallas_call x1, Pallas kernels, turn(): pl.pallas_call(turn_kernel, name='turn', grid_spec=pltpu.PrefetchScalarGr...  15.5 us
    ppermute x4, starting transfers between devices, step(): part[m] = lax.ppermute(part[m], 'ep', across)  6.88 us
    convert_element_type x5, other arithmetic, finish(): return (h[m].astype(F32) + near[m] + part[m]).astype(BF16)  6.19 us
    ppermute x4, starting transfers between devices, step(): u.append(lax.ppermute(y, 'pp', perm))  5.37 us
  transfers between devices with their start and end apart: 22, of which 7 were waited for; matrix products, arithmetic and copies ran while one was open for 2% of the time, Pallas kernels for 43%

profile of v1, /device:TPU:0, one launch (start us, length us, event | category | flops | bytes accessed | tf_op | source)
XLA Modules:
  0.0 195.3 jit_solution(8252380910847394729)
XLA Ops:
  0.0 49.6 %front.1 = (f32[128,1792]{1,0:T(8,128)}, f32[128,1792]{1,0:T(8,128)}, f32[128,1792]{1,0:T(8,128)}, f32[128,1792]{1,0:T(8,128)}, f32[128,1792]{1,0:T(8,128)}, /*i...) custom-call(s32[6,8,128]{2,1,0:T(8,128)} %bitcast.77, s32[6,8,128]{2,1,0:T(8,128)} %bitcast.78, f32[6,8,128]{2,1,0:T(8,128)} %bitcast.79, ...), custom_call_target="tpu_custom_call" | custom-call | flops 12683575296 | tf_op jit(solution)/shard_map/front/pallas_call | solution.py:120
  49.7 3.2 %fusion.9 = (bf16[128,1792]{1,0:T(8,128)(2,1)}, bf16[128,1792]{1,0:T(8,128)(2,1)}) fusion(f32[128,1792]{1,0:T(8,128)} %get-tuple-element.77, f32[6,128,1792]{2,1,0:T(8,128)} %get-tuple-element.121, bf16[1,6,1,128,1792]{4,3,2,1,0:T(8,128)(2,1)S(1)} %copy-done.2, f32[128,1792]{1,0:T(8,128)} %get-tuple-element.76), kind=kLoop, calls=%fused_computation.14 | loop fusion | flops 1835008 | bytes 5505024 | tf_op jit(solution)/shard_map/convert_element_type | solution.py:255
  52.8 1.9 collective-permute-start
  54.8 1.5 collective-permute-start.1
  56.3 15.5 %turn.1 = (bf16[16,1792,128]{2,1,0:T(8,128)(2,1)S(1)}, bf16[16,1792,128]{2,1,0:T(8,128)(2,1)S(1)}, bf16[16,1792,128]{2,1,0:T(8,128)(2,1)S(1)}, bf16[16,128,1792]{2,1,0:T(8,128)(2,1)S(1)}) custom-call(s32[1]{0:T(128)} %bitcast.16.c_ref, bf16[1792,32,128]{2,1,0:T(8,128)(2,1)} %bitcast.72, bf16[1792,32,128]{2,1,0:T(8,128)(2,1)} %bitcast.73, ...), custom_call_target="tpu_custom_call" | custom-call | flops 10000000000 | bytes 29360128 | tf_op jit(solution)/shard_map/turn/pallas_call | solution.py:172
  71.8 0.0 copy-start.3
  71.9 0.0 copy-start
  71.9 4.5 %collective-permute-done.1 = f32[128,1792]{1,0:T(8,128)} collective-permute-done((f32[128,1792]{1,0:T(8,128)}, f32[128,1792]{1,0:T(8,128)}, u32[]{:S(2)}, u32[]{:S(2)}) %collective-permute-start.1) | collective-permute-done | bytes 917536 | tf_op jit(solution)/shard_map/ppermute | solution.py:249
  76.4 1.3 fusion.7
  77.7 0.0 collective-permute-done.u_ref
  77.7 0.1 collective-permute-start.2
  77.8 1.6 collective-permute-start.4
  79.5 1.7 collective-permute-start.5
  81.2 0.0 collective-permute-done.2.v_ref
  81.2 11.5 %layer.6 = (f32[128,1792]{1,0:T(8,128)S(1)}, f32[128,1792]{1,0:T(8,128)S(1)}) custom-call(bf16[128,1792]{1,0:T(8,128)(2,1)S(1)} %collective-permute-done.u_ref, bf16[128,1792]{1,0:T(8,128)(2,1)S(1)} %collective-permute-done.2.v_ref, f32[1,1792]{1,0:T(1,128)S(1)} %copy-done, bf16[16,1792,128]{2,1,0:T(8,128)(2,1)S(1)} %get-tuple-element.91.q_ref, ...), custom_call_target="tpu_custom_call" | custom-call | flops 15032385536 | bytes 29360128 | tf_op jit(solution)/shard_map/layer/pallas_call | solution.py:221
  92.7 9.2 %collective-permute-done.5 = f32[128,1792]{1,0:T(8,128)S(1)} collective-permute-done((f32[128,1792]{1,0:T(8,128)S(1)}, f32[128,1792]{1,0:T(8,128)S(1)}, u32[]{:S(2)}, u32[]{:S(2)}) %collective-permute-start.5) | collective-permute-done | bytes 917536 | tf_op jit(solution)/shard_map/ppermute | solution.py:249
  101.9 0.2 fusion.5
  102.0 0.0 collective-permute-done.4.u_ref
  102.1 0.1 collective-permute-start.6
  102.1 1.8 collective-permute-start.9
  104.0 1.6 collective-permute-start.8
  105.5 0.0 collective-permute-start.3
  105.5 0.0 collective-permute-done.6.v_ref
  105.5 11.5 %layer.7 = (f32[128,1792]{1,0:T(8,128)S(1)}, f32[128,1792]{1,0:T(8,128)S(1)}) custom-call(bf16[128,1792]{1,0:T(8,128)(2,1)S(1)} %collective-permute-done.4.u_ref, bf16[128,1792]{1,0:T(8,128)(2,1)S(1)} %collective-permute-done.6.v_ref, f32[1,1792]{1,0:T(1,128)S(1)} %copy-done, bf16[16,1792,128]{2,1,0:T(8,128)(2,1)S(1)} %get-tuple-element.91.q_ref, ...), custom_call_target="tpu_custom_call" | custom-call | flops 15032385536 | bytes 29360128 | tf_op jit(solution)/shard_map/layer/pallas_call | solution.py:221
  117.0 7.9 %collective-permute-done.9 = f32[128,1792]{1,0:T(8,128)S(1)} collective-permute-done((f32[128,1792]{1,0:T(8,128)S(1)}, f32[128,1792]{1,0:T(8,128)S(1)}, u32[]{:S(2)}, u32[]{:S(2)}) %collective-permute-start.9) | collective-permute-done | bytes 917536 | tf_op jit(solution)/shard_map/ppermute | solution.py:249
  124.9 0.2 fusion.3
  125.1 0.0 collective-permute-done.8.u_ref
  125.1 0.1 collective-permute-start.10
  125.1 1.8 collective-permute-start.13
  127.0 1.6 collective-permute-start.12
  128.5 0.4 collective-permute-start.16
  128.9 0.0 collective-permute-done.3
  128.9 0.0 collective-permute-start.7
  128.9 0.0 collective-permute-done.10.v_ref
  128.9 11.4 %layer.8 = (f32[128,1792]{1,0:T(8,128)S(1)}, f32[128,1792]{1,0:T(8,128)S(1)}) custom-call(bf16[128,1792]{1,0:T(8,128)(2,1)S(1)} %collective-permute-done.8.u_ref, bf16[128,1792]{1,0:T(8,128)(2,1)S(1)} %collective-permute-done.10.v_ref, f32[1,1792]{1,0:T(1,128)S(1)} %copy-done, bf16[16,1792,128]{2,1,0:T(8,128)(2,1)S(1)} %get-tuple-element.91.q_ref, ...), custom_call_target="tpu_custom_call" | custom-call | flops 15032385536 | bytes 29360128 | tf_op jit(solution)/shard_map/layer/pallas_call | solution.py:221
  140.4 7.8 %collective-permute-done.13 = f32[128,1792]{1,0:T(8,128)} collective-permute-done((f32[128,1792]{1,0:T(8,128)}, f32[128,1792]{1,0:T(8,128)}, u32[]{:S(2)}, u32[]{:S(2)}) %collective-permute-start.13) | collective-permute-done | bytes 917536 | tf_op jit(solution)/shard_map/ppermute | solution.py:249
  148.2 1.3 fusion.1
  149.6 0.0 collective-permute-done.12.u_ref
  149.6 1.8 collective-permute-start.19
  151.4 0.0 collective-permute-start.14
  151.4 0.5 collective-permute-start.11
  151.9 0.0 collective-permute-done.16.u_ref
  151.9 0.0 collective-permute-start.17
  151.9 0.2 fusion.13
  152.1 1.1 collective-permute-done.14.v_ref
  153.2 11.4 %layer.9 = (f32[128,1792]{1,0:T(8,128)S(1)}, f32[128,1792]{1,0:T(8,128)S(1)}) custom-call(bf16[128,1792]{1,0:T(8,128)(2,1)S(1)} %collective-permute-done.12.u_ref, bf16[128,1792]{1,0:T(8,128)(2,1)S(1)} %collective-permute-done.14.v_ref, f32[1,1792]{1,0:T(1,128)S(1)} %copy-done, bf16[16,1792,128]{2,1,0:T(8,128)(2,1)S(1)} %get-tuple-element.91.q_ref, ...), custom_call_target="tpu_custom_call" | custom-call | flops 15032385536 | bytes 29360128 | tf_op jit(solution)/shard_map/layer/pallas_call | solution.py:221
  164.7 0.0 collective-permute-done.7
  164.7 0.2 collective-permute-start.15
  164.9 0.0 collective-permute-done.17.v_ref
  164.9 11.5 %layer.10 = (f32[128,1792]{1,0:T(8,128)S(1)}, f32[128,1792]{1,0:T(8,128)S(1)}) custom-call(bf16[128,1792]{1,0:T(8,128)(2,1)S(1)} %collective-permute-done.16.u_ref, bf16[128,1792]{1,0:T(8,128)(2,1)S(1)} %collective-permute-done.17.v_ref, f32[1,1792]{1,0:T(1,128)S(1)} %copy-done, bf16[16,1792,128]{2,1,0:T(8,128)(2,1)S(1)} %get-tuple-element.91.q_ref, ...), custom_call_target="tpu_custom_call" | custom-call | flops 15032385536 | bytes 29360128 | tf_op jit(solution)/shard_map/layer/pallas_call | solution.py:221
  176.4 0.4 collective-permute-start.18
  176.8 0.2 collective-permute-start.20
  177.0 0.1 fusion.15
  177.1 2.5 %collective-permute-done.20.v_ref = bf16[128,1792]{1,0:T(8,128)(2,1)S(1)} collective-permute-done((bf16[128,1792]{1,0:T(8,128)(2,1)S(1)}, bf16[128,1792]{1,0:T(8,128)(2,1)S(1)}, u32[]{:S(2)}, u32[]{:S(2)}) %collective-permute-start.20) | collective-permute-done | bytes 458784 | tf_op jit(solution)/shard_map/ppermute | solution.py:258
  179.6 11.5 %layer.11 = (f32[128,1792]{1,0:T(8,128)S(1)}, f32[128,1792]{1,0:T(8,128)S(1)}) custom-call(bf16[128,1792]{1,0:T(8,128)(2,1)S(1)} %collective-permute-done.19.u_ref, bf16[128,1792]{1,0:T(8,128)(2,1)S(1)} %collective-permute-done.20.v_ref, f32[1,1792]{1,0:T(1,128)S(1)} %copy-done, bf16[16,1792,128]{2,1,0:T(8,128)(2,1)S(1)} %get-tuple-element.91.q_ref, ...), custom_call_target="tpu_custom_call" | custom-call | flops 15032385536 | bytes 29360128 | tf_op jit(solution)/shard_map/layer/pallas_call | solution.py:221
  191.1 0.4 collective-permute-start.21
  191.5 0.1 fusion.17
  191.6 0.0 collective-permute-done.15
  191.6 0.1 fusion.19
  191.8 0.1 fusion.21
  191.9 1.7 collective-permute-done.21
  193.6 0.1 fusion.23
  193.7 0.0 copy-start.4
  193.7 1.5 copy-done.4
  (13 shorter events, 0.0 us)
Async XLA Ops:
  0.0 49.7 %copy-start.2 = (bf16[1,6,1,128,1792]{4,3,2,1,0:T(8,128)(2,1)S(1)}, bf16[1,6,1,128,1792]{4,3,2,1,0:T(8,128)(2,1)}, u32[]{:S(2)}) copy-start(bf16[1,6,1,128,1792]{4,3,2,1,0:T(8,128)(2,1)} %param.14) | copy-start | bytes 8257540
  52.8 24.9 %collective-permute-start = (bf16[128,1792]{1,0:T(8,128)(2,1)}, bf16[128,1792]{1,0:T(8,128)(2,1)S(1)}, u32[]{:S(2)}, u32[]{:S(2)}) collective-permute-start(bf16[128,1792]{1,0:T(8,128)(2,1)} %get-tuple-element.78), channel_id=1, source_target_pairs={{0,4},{4,8},{8,12},{12,0},{1,5},{5,9},{9,13},{13,1},{2,6},{6,10},{... | collective-permute-start | bytes 1376264 | tf_op jit(solution)/shard_map/ppermute | solution.py:266
  54.8 21.6 %collective-permute-start.1 = (f32[128,1792]{1,0:T(8,128)}, f32[128,1792]{1,0:T(8,128)}, u32[]{:S(2)}, u32[]{:S(2)}) collective-permute-start(f32[128,1792]{1,0:T(8,128)} %get-tuple-element.89), channel_id=1, source_target_pairs={{0,2},{1,3},{2,0},{3,1},{4,6},{5,7},{6,4},{7,5},{8,10},{9,11},{10,... | collective-permute-start | bytes 2752520 | tf_op jit(solution)/shard_map/ppermute | solution.py:249
  56.3 20.1 %copy-start.1 = (f32[6,128,1792]{2,1,0:T(8,128)S(1)}, f32[6,128,1792]{2,1,0:T(8,128)}, u32[]{:S(2)}) copy-start(f32[6,128,1792]{2,1,0:T(8,128)} %get-tuple-element.121) | copy-start | bytes 16515076
  71.8 6.0 %copy-start.3 = (bf16[128,1792]{1,0:T(8,128)(2,1)S(1)}, bf16[128,1792]{1,0:T(8,128)(2,1)}, u32[]{:S(2)}) copy-start(bf16[128,1792]{1,0:T(8,128)(2,1)} %get-tuple-element.98) | copy-start | bytes 1376260
  71.9 7.6 %copy-start.6 = (f32[128,1792]{1,0:T(8,128)S(1)}, f32[128,1792]{1,0:T(8,128)}, u32[]{:S(2)}) copy-start(f32[128,1792]{1,0:T(8,128)} %get-tuple-element.100) | copy-start | bytes 2752516
  71.9 9.3 %copy-start = (f32[1,1792]{1,0:T(1,128)S(1)}, f32[1,1792]{1,0:T(1,128)}, u32[]{:S(2)}) copy-start(f32[1,1792]{1,0:T(1,128)} %w_ref.11) | copy-start | bytes 21508
  77.7 3.5 %collective-permute-start.2 = (bf16[128,1792]{1,0:T(8,128)(2,1)S(1)}, bf16[128,1792]{1,0:T(8,128)(2,1)S(1)}, u32[]{:S(2)}, u32[]{:S(2)}) collective-permute-start(bf16[128,1792]{1,0:T(8,128)(2,1)S(1)} %collective-permute-done.u_ref), channel_id=1, source_target_pairs={{0,1},{1,0},{2,3},{3,2},{4,5},{5,4},{6,7},{7,6},{8,9},{9,8},{10,11... | collective-permute-start | bytes 1376264 | tf_op jit(solution)/shard_map/ppermute | solution.py:258
  77.8 24.2 %collective-permute-start.4 = (bf16[128,1792]{1,0:T(8,128)(2,1)S(1)}, bf16[128,1792]{1,0:T(8,128)(2,1)S(1)}, u32[]{:S(2)}, u32[]{:S(2)}) collective-permute-start(bf16[128,1792]{1,0:T(8,128)(2,1)S(1)} %copy-done.3), channel_id=1, source_target_pairs={{0,4},{4,8},{8,12},{12,0},{1,5},{5,9},{9,13},{13,1},{2,6},{6,10},{... | collective-permute-start | bytes 1376264 | tf_op jit(solution)/shard_map/ppermute | solution.py:266
  79.5 22.4 %collective-permute-start.5 = (f32[128,1792]{1,0:T(8,128)S(1)}, f32[128,1792]{1,0:T(8,128)S(1)}, u32[]{:S(2)}, u32[]{:S(2)}) collective-permute-start(f32[128,1792]{1,0:T(8,128)S(1)} %copy-done.6), channel_id=1, source_target_pairs={{0,2},{1,3},{2,0},{3,1},{4,6},{5,7},{6,4},{7,5},{8,10},{9,11},{10,... | collective-permute-start | bytes 2752520 | tf_op jit(solution)/shard_map/ppermute | solution.py:249
  92.7 9.4 %copy-start.5 = (f32[128,1792]{1,0:T(8,128)S(1)}, f32[128,1792]{1,0:T(8,128)}, u32[]{:S(2)}) copy-start(f32[128,1792]{1,0:T(8,128)} %get-tuple-element.111) | copy-start | bytes 2752516
  102.1 3.5 %collective-permute-start.6 = (bf16[128,1792]{1,0:T(8,128)(2,1)S(1)}, bf16[128,1792]{1,0:T(8,128)(2,1)S(1)}, u32[]{:S(2)}, u32[]{:S(2)}) collective-permute-start(bf16[128,1792]{1,0:T(8,128)(2,1)S(1)} %collective-permute-done.4.u_ref), channel_id=1, source_target_pairs={{0,1},{1,0},{2,3},{3,2},{4,5},{5,4},{6,7},{7,6},{8,9},{9,8},{10,11... | collective-permute-start | bytes 1376264 | tf_op jit(solution)/shard_map/ppermute | solution.py:258
  102.1 22.7 %collective-permute-start.9 = (f32[128,1792]{1,0:T(8,128)S(1)}, f32[128,1792]{1,0:T(8,128)S(1)}, u32[]{:S(2)}, u32[]{:S(2)}) collective-permute-start(f32[128,1792]{1,0:T(8,128)S(1)} %copy-done.5), channel_id=1, source_target_pairs={{0,2},{1,3},{2,0},{3,1},{4,6},{5,7},{6,4},{7,5},{8,10},{9,11},{10,... | collective-permute-start | bytes 2752520 | tf_op jit(solution)/shard_map/ppermute | solution.py:249
  104.0 21.1 %collective-permute-start.8 = (bf16[128,1792]{1,0:T(8,128)(2,1)S(1)}, bf16[128,1792]{1,0:T(8,128)(2,1)S(1)}, u32[]{:S(2)}, u32[]{:S(2)}) collective-permute-start(bf16[128,1792]{1,0:T(8,128)(2,1)S(1)} %fusion.7), channel_id=1, source_target_pairs={{0,4},{4,8},{8,12},{12,0},{1,5},{5,9},{9,13},{13,1},{2,6},{6,10},{... | collective-permute-start | bytes 1376264 | tf_op jit(solution)/shard_map/ppermute | solution.py:275
  105.5 23.4 %collective-permute-start.3 = (f32[128,1792]{1,0:T(8,128)S(1)}, f32[128,1792]{1,0:T(8,128)S(1)}, u32[]{:S(2)}, u32[]{:S(2)}) collective-permute-start(f32[128,1792]{1,0:T(8,128)S(1)} %get-tuple-element.97), channel_id=1, source_target_pairs={{0,1},{1,0},{2,3},{3,2},{4,5},{5,4},{6,7},{7,6},{8,9},{9,8},{10,11... | collective-permute-start | bytes 2752520 | tf_op jit(solution)/shard_map/ppermute | solution.py:259
  125.1 3.9 %collective-permute-start.10 = (bf16[128,1792]{1,0:T(8,128)(2,1)S(1)}, bf16[128,1792]{1,0:T(8,128)(2,1)S(1)}, u32[]{:S(2)}, u32[]{:S(2)}) collective-permute-start(bf16[128,1792]{1,0:T(8,128)(2,1)S(1)} %collective-permute-done.8.u_ref), channel_id=1, source_target_pairs={{0,1},{1,0},{2,3},{3,2},{4,5},{5,4},{6,7},{7,6},{8,9},{9,8},{10,11... | collective-permute-start | bytes 1376264 | tf_op jit(solution)/shard_map/ppermute | solution.py:258
  125.1 23.1 %collective-permute-start.13 = (f32[128,1792]{1,0:T(8,128)}, f32[128,1792]{1,0:T(8,128)}, u32[]{:S(2)}, u32[]{:S(2)}) collective-permute-start(f32[128,1792]{1,0:T(8,128)} %get-tuple-element.122), channel_id=1, source_target_pairs={{0,2},{1,3},{2,0},{3,1},{4,6},{5,7},{6,4},{7,5},{8,10},{9,11},{10,... | collective-permute-start | bytes 2752520 | tf_op jit(solution)/shard_map/ppermute | solution.py:249
  127.0 22.6 %collective-permute-start.12 = (bf16[128,1792]{1,0:T(8,128)(2,1)S(1)}, bf16[128,1792]{1,0:T(8,128)(2,1)S(1)}, u32[]{:S(2)}, u32[]{:S(2)}) collective-permute-start(bf16[128,1792]{1,0:T(8,128)(2,1)S(1)} %fusion.5), channel_id=1, source_target_pairs={{0,4},{4,8},{8,12},{12,0},{1,5},{5,9},{9,13},{13,1},{2,6},{6,10},{... | collective-permute-start | bytes 1376264 | tf_op jit(solution)/shard_map/ppermute | solution.py:275
  128.5 23.4 %collective-permute-start.16 = (bf16[128,1792]{1,0:T(8,128)(2,1)S(1)}, bf16[128,1792]{1,0:T(8,128)(2,1)S(1)}, u32[]{:S(2)}, u32[]{:S(2)}) collective-permute-start(bf16[128,1792]{1,0:T(8,128)(2,1)S(1)} %fusion.3), channel_id=1, source_target_pairs={{0,4},{4,8},{8,12},{12,0},{1,5},{5,9},{9,13},{13,1},{2,6},{6,10},{... | collective-permute-start | bytes 1376264 | tf_op jit(solution)/shard_map/ppermute | solution.py:275
  128.9 35.8 %collective-permute-start.7 = (f32[128,1792]{1,0:T(8,128)S(1)}, f32[128,1792]{1,0:T(8,128)S(1)}, u32[]{:S(2)}, u32[]{:S(2)}) collective-permute-start(f32[128,1792]{1,0:T(8,128)S(1)} %get-tuple-element.108), channel_id=1, source_target_pairs={{0,1},{1,0},{2,3},{3,2},{4,5},{5,4},{6,7},{7,6},{8,9},{9,8},{10,11... | collective-permute-start | bytes 2752520 | tf_op jit(solution)/shard_map/ppermute | solution.py:259
  149.6 27.2 %collective-permute-start.19 = (bf16[128,1792]{1,0:T(8,128)(2,1)S(1)}, bf16[128,1792]{1,0:T(8,128)(2,1)S(1)}, u32[]{:S(2)}, u32[]{:S(2)}) collective-permute-start(bf16[128,1792]{1,0:T(8,128)(2,1)S(1)} %fusion.1), channel_id=1, source_target_pairs={{0,4},{4,8},{8,12},{12,0},{1,5},{5,9},{9,13},{13,1},{2,6},{6,10},{... | collective-permute-start | bytes 1376264 | tf_op jit(solution)/shard_map/ppermute | solution.py:275
  151.4 1.8 collective-permute-start.14
  151.4 39.7 %collective-permute-start.11 = (f32[128,1792]{1,0:T(8,128)S(1)}, f32[128,1792]{1,0:T(8,128)S(1)}, u32[]{:S(2)}, u32[]{:S(2)}) collective-permute-start(f32[128,1792]{1,0:T(8,128)S(1)} %get-tuple-element.119), channel_id=1, source_target_pairs={{0,1},{1,0},{2,3},{3,2},{4,5},{5,4},{6,7},{7,6},{8,9},{9,8},{10,11... | collective-permute-start | bytes 2752520 | tf_op jit(solution)/shard_map/ppermute | solution.py:259
  151.9 13.0 %collective-permute-start.17 = (bf16[128,1792]{1,0:T(8,128)(2,1)S(1)}, bf16[128,1792]{1,0:T(8,128)(2,1)S(1)}, u32[]{:S(2)}, u32[]{:S(2)}) collective-permute-start(bf16[128,1792]{1,0:T(8,128)(2,1)S(1)} %collective-permute-done.16.u_ref), channel_id=1, source_target_pairs={{0,1},{1,0},{2,3},{3,2},{4,5},{5,4},{6,7},{7,6},{8,9},{9,8},{10,11... | collective-permute-start | bytes 1376264 | tf_op jit(solution)/shard_map/ppermute | solution.py:258
  164.7 26.9 %collective-permute-start.15 = (f32[128,1792]{1,0:T(8,128)S(1)}, f32[128,1792]{1,0:T(8,128)S(1)}, u32[]{:S(2)}, u32[]{:S(2)}) collective-permute-start(f32[128,1792]{1,0:T(8,128)S(1)} %get-tuple-element.130), channel_id=1, source_target_pairs={{0,1},{1,0},{2,3},{3,2},{4,5},{5,4},{6,7},{7,6},{8,9},{9,8},{10,11... | collective-permute-start | bytes 2752520 | tf_op jit(solution)/shard_map/ppermute | solution.py:259
  176.4 15.2 %collective-permute-start.18 = (f32[128,1792]{1,0:T(8,128)S(1)}, f32[128,1792]{1,0:T(8,128)S(1)}, u32[]{:S(2)}, u32[]{:S(2)}) collective-permute-start(f32[128,1792]{1,0:T(8,128)S(1)} %get-tuple-element.137), channel_id=1, source_target_pairs={{0,1},{1,0},{2,3},{3,2},{4,5},{5,4},{6,7},{7,6},{8,9},{9,8},{10,11... | collective-permute-start | bytes 2752520 | tf_op jit(solution)/shard_map/ppermute | solution.py:259
  176.8 2.8 %collective-permute-start.20 = (bf16[128,1792]{1,0:T(8,128)(2,1)S(1)}, bf16[128,1792]{1,0:T(8,128)(2,1)S(1)}, u32[]{:S(2)}, u32[]{:S(2)}) collective-permute-start(bf16[128,1792]{1,0:T(8,128)(2,1)S(1)} %collective-permute-done.19.u_ref), channel_id=1, source_target_pairs={{0,1},{1,0},{2,3},{3,2},{4,5},{5,4},{6,7},{7,6},{8,9},{9,8},{10,11... | collective-permute-start | bytes 1376264 | tf_op jit(solution)/shard_map/ppermute | solution.py:258
  191.1 2.5 %collective-permute-start.21 = (f32[128,1792]{1,0:T(8,128)S(1)}, f32[128,1792]{1,0:T(8,128)S(1)}, u32[]{:S(2)}, u32[]{:S(2)}) collective-permute-start(f32[128,1792]{1,0:T(8,128)S(1)} %get-tuple-element.144), channel_id=1, source_target_pairs={{0,1},{1,0},{2,3},{3,2},{4,5},{5,4},{6,7},{7,6},{8,9},{9,8},{10,11... | collective-permute-start | bytes 2752520 | tf_op jit(solution)/shard_map/ppermute | solution.py:259
  193.7 1.5 copy-start.4
